TPU v7x, 256 devices: a whole 4x4x8 slice. The times are simulated.
256 devices in a mesh: expert: 8 (over z), tp: 32 (over x, y, core).
Axes of the slice: x: 4, y: 4, z: 8, core: 2. Of those that a mesh axis runs over, the one named last changes fastest.
Arguments:
- tokens: bfloat16 [1024, 4096], P('expert', 'tp'), may hold values from -6 to 6
- norm_gain: bfloat16 [4096], replicated, may hold values from 0.5 to 1.5
- route_logits: float32 [1024, 2], P('expert'), may hold values from -6 to 6
- expert_ids: int32 [1024, 2], P('expert'), may hold values from 0 to 7, all different within a row; in each aligned block of 128 rows (0 to 127, 128 to 255, ...) at most 64 rows name the same one
- active: int32 [1024], P('expert'), may hold values 0 or 1
- gate_weight: bfloat16 [8, 14336, 4096], P('expert', 'tp'), may hold values from -0.09375 to 0.09375
- up_weight: bfloat16 [8, 14336, 4096], P('expert', 'tp'), may hold values from -0.09375 to 0.09375
- down_weight: bfloat16 [8, 14336, 4096], P('expert', 'tp'), may hold values from -0.046875 to 0.046875
Outputs:
- mixed: bfloat16 [1024, 4096], P('expert', 'tp')
Inputs may be any that keep to these rules, and one draw needn't show every extreme that they name: `expert_ids`: each token names 2 different experts. In each block of 128 consecutive token slots (the slots of one index of expert) no expert is named by more than 64 tokens, a bound that some block reaches. `active`: each entry is 0 or 1.
All inputs are finite; a program needn't handle non-finite values.
Results may differ from a plain program's by a relative error of at most 0.0025.
Values may be sent and summed in bfloat16 or wider, within the bound.
A program may use at most 64 MiB of HBM per device.

v0:
```python
import jax
import jax.numpy as jnp
from jax import lax
from jax.sharding import Mesh
from jax.sharding import PartitionSpec as P

TP = ("tp_0", "tp_1", "tp_2")
epsilon = 1e-05


def one_axis_at_a_time(shard, axes):
    for axis in axes:
        shard = lax.psum(shard, axis)
    return shard


def taken_in(shard, axis, dim, absorb, state):
    everything = jax.tree.map(lambda a: lax.all_gather(a, axis, axis=dim, tiled=True), shard)
    return absorb(state, everything, jnp.int32(0))


def own_rows(product, width, axis):
    everything = product(jnp.int32(0), lax.axis_size(axis) * width)
    own = lax.psum_scatter(everything, axis, scatter_dimension=0, tiled=True)
    return own


def slot_numbers(expert_ids, active, seat_limit, experts):
    flat_ids = expert_ids.reshape(-1)
    is_live = jnp.broadcast_to(active[:, None], expert_ids.shape).reshape(-1)
    columns = jnp.arange(experts, dtype=jnp.int32)
    one_hot = (flat_ids[:, None] == columns[None, :]).astype(jnp.int32) * is_live[:, None]
    earlier = jnp.cumsum(one_hot, axis=0) - one_hot
    position = jnp.sum(earlier * one_hot, axis=1)
    slot_index = jnp.where(is_live > 0, flat_ids * seat_limit + position, -1)
    return slot_index.reshape(expert_ids.shape)


def local(tokens, norm_gain, route_logits, expert_ids, active, gate_weight, up_weight, down_weight):
    expert_count = lax.axis_size("expert")
    tp_index = lax.axis_index(TP)
    token_count, feature_share = tokens.shape
    local_count, ff_share, model_width = gate_weight.shape
    seat_limit = token_count // 2
    experts = expert_count * local_count
    slots = expert_count * seat_limit
    gains = norm_gain.astype(jnp.float32)
    widened = tokens.astype(jnp.float32)
    squares = one_axis_at_a_time(jnp.sum(widened * widened, axis=1), TP)
    gain_part = lax.dynamic_slice_in_dim(gains, tp_index * feature_share, feature_share)
    mean_square = squares[:, None] / model_width
    normed = (widened * lax.rsqrt(mean_square + epsilon) * gain_part).astype(jnp.bfloat16)
    route_probs = jax.nn.softmax(route_logits, axis=1) * active.astype(jnp.float32)[:, None]
    slot_index = slot_numbers(expert_ids, active, seat_limit, experts)
    buffer_rows = experts * seat_limit
    targets = jnp.arange(buffer_rows, dtype=jnp.int32)
    pick_hot = (slot_index[:, :, None] == targets[None, None, :]).astype(jnp.bfloat16)
    send_hot = jnp.sum(pick_hot, axis=1)
    send_rows = jnp.einsum(
        "jr,jw->rw", send_hot, normed, preferred_element_type=jnp.float32
    ).astype(jnp.bfloat16)
    arriving = lax.all_to_all(send_rows, "expert", split_axis=0, concat_axis=0, tiled=True)
    received = arriving.reshape(expert_count, local_count, seat_limit, -1).transpose(1, 0, 2, 3)
    received = received.reshape(local_count, slots, -1)
    empty = jnp.zeros((local_count, slots, ff_share), jnp.float32)

    def add_projections(running, shard_piece, offset):
        sequence_extent = shard_piece.shape[2]
        gate_part = lax.dynamic_slice_in_dim(gate_weight, offset, sequence_extent, 2)
        up_part = lax.dynamic_slice_in_dim(up_weight, offset, sequence_extent, 2)
        gate_next = running[0] + jnp.einsum(
            "lrd,lfd->lrf", shard_piece, gate_part, preferred_element_type=jnp.float32
        )
        up_next = running[1] + jnp.einsum(
            "lrd,lfd->lrf", shard_piece, up_part, preferred_element_type=jnp.float32
        )
        return (gate_next, up_next)

    gate_sum, up_sum = taken_in(received, TP, 2, add_projections, (empty, empty))
    inner_width = (jax.nn.silu(gate_sum) * up_sum).astype(jnp.bfloat16)

    def down_terms(offset, count):
        lowering_share = lax.dynamic_slice_in_dim(down_weight, offset, count, 2)
        return jnp.einsum(
            "hzj,hjs->shz", inner_width, lowering_share, preferred_element_type=jnp.float32
        )

    reduced = own_rows(down_terms, feature_share, TP)
    specialist_result = reduced.transpose(1, 2, 0).astype(jnp.bfloat16)
    returning = specialist_result.reshape(
        local_count, expert_count, seat_limit, feature_share
    ).transpose(1, 0, 2, 3)
    returning = returning.reshape(expert_count * local_count * seat_limit, feature_share)
    arrived = lax.all_to_all(returning, "expert", split_axis=0, concat_axis=0, tiled=True)
    picked = jnp.einsum("jkr,rw->jkw", pick_hot, arrived, preferred_element_type=jnp.float32)
    mixed = jnp.sum(route_probs[:, :, None] * picked, axis=1)
    return mixed.astype(jnp.bfloat16)


def solution(mesh):
    split = Mesh(
        mesh.devices.reshape(mesh.shape["expert"], 4, 4, 2), ("expert", "tp_0", "tp_1", "tp_2")
    )
    in_specs = (
        P("expert", TP),
        P(),
        P("expert", None),
        P("expert", None),
        P("expert"),
        P("expert", TP, None),
        P("expert", TP, None),
        P("expert", TP, None),
    )
    out_specs = P("expert", TP)
    return jax.shard_map(local, mesh=split, in_specs=in_specs, out_specs=out_specs, check_vma=False)
```

profile of v0, /device:TPU:2, one launch (start us, length us, event | category | flops | bytes accessed | tf_op | source)
XLA Modules:
  0.0 244.5 jit_solution(12486279213063765660)
XLA Ops:
  6.5 0.8 copy.19
  7.3 0.1 eq.38
  7.5 0.1 eq.42
  7.6 0.7 broadcast_in_dim.27
  8.3 0.7 broadcast_compare_fusion
  9.0 0.1 broadcast_in_dim.28
  9.1 0.1 broadcast_in_dim.29
  9.2 0.6 reduce-window.6
  9.8 0.2 slice_reduce_fusion
  10.1 0.7 broadcast_in_dim.30
  10.8 0.1 mul.85
  11.0 0.1 fusion.36
  11.1 0.1 reduce_sum.52
  11.2 0.1 copy.21
  11.3 0.7 add_select_fusion
  12.0 0.1 fusion.28
  12.1 0.9 fusion.30
  13.0 10.0 %psum.21 = f32[128]{0:T(128)S(1)} all-reduce(f32[128]{0:T(128)S(1)} %fusion.30), channel_id=1, replica_groups=mesh['expert'=8,'tp_0'=4,'tp_1'=4,'tp_2'=2] {'tp_0'}, use_global_device_ids=true, to_apply=%region_7.8 | all-reduce | flops 128 | bytes 1024 | tf_op jit(solution)/shard_map/psum | solution.py:13
  22.9 9.4 %psum.22 = f32[128]{0:T(128)S(1)} all-reduce(f32[128]{0:T(128)S(1)} %psum.21), channel_id=1, replica_groups=mesh['expert'=8,'tp_0'=4,'tp_1'=4,'tp_2'=2] {'tp_1'}, use_global_device_ids=true, to_apply=%region_8.9 | all-reduce | flops 128 | bytes 1024 | tf_op jit(solution)/shard_map/psum | solution.py:13
  32.3 2.5 %psum.23 = f32[128]{0:T(128)S(1)} all-reduce(f32[128]{0:T(128)S(1)} %psum.22), channel_id=1, replica_groups=mesh['expert'=8,'tp_0'=4,'tp_1'=4,'tp_2'=2] {'tp_2'}, use_global_device_ids=true, to_apply=%region_9.10 | all-reduce | flops 128 | bytes 1024 | tf_op jit(solution)/shard_map/psum | solution.py:13
  34.8 0.8 dynamic-slice_convert_fusion
  35.5 1.0 convolution_convert_fusion
  36.5 17.8 %all_to_all.21 = bf16[8,64,128]{2,1,0:T(8,128)(2,1)} all-to-all(bf16[8,64,128]{2,1,0:T(8,128)(2,1)S(1)} %bitcast.45), channel_id=1, replica_groups=mesh['expert'=8,'tp_0'=4,'tp_1'=4,'tp_2'=2] {'expert'}, dimensions={0} | all-to-all | bytes 262144 | tf_op jit(solution)/shard_map/all_to_all | solution.py:62
  54.4 47.1 %all-gather.2.cloned.1.call-done = bf16[1,512,4096]{2,1,0:T(8,128)(2,1)} async-done(((bf16[1,512,128]{2,1,0:T(8,128)(2,1)}), bf16[1,512,4096]{2,1,0:T(8,128)(2,1)}) %all-gather.2.cloned.1.call-update) | async-done | bytes 4194320 | tf_op jit(solution)/shard_map/all_gather | solution.py:18
  101.5 5.4 %fusion.2 = f32[512,448]{0,1:T(8,128)S(1)} fusion(bf16[1,512,4096]{2,1,0:T(8,128)(2,1)} %all-gather.2.cloned.1.call-done, bf16[1,448,4096]{2,1,0:T(8,128)(2,1)} %param.13), kind=kOutput, calls=%fused_computation.3 | convolution fusion | flops 1879048192 | bytes 8781824 | tf_op jit(solution)/shard_map/lrd,lfd->lrf/dot_general | solution.py:71
  106.9 12.0 %convolution_bitcast_fusion = f32[4096,1,512]{0,2,1:T(8,128)} fusion(bf16[1,448,4096]{2,1,0:T(8,128)(2,1)} %param.15, bf16[1,448,4096]{2,1,0:T(8,128)(2,1)} %param.14, bf16[1,512,4096]{2,1,0:T(8,128)(2,1)} %all-gather.2.cloned.1.call-done, f32[512,448]{0,1:T(8,128)S(1)} %fusion.2), kind=kOutput, calls=%fused_computation | convolution fusion | flops 3759472640 | bytes 20840448 | tf_op jit(solution)/shard_map/hzj,hjs->shz/dot_general | solution.py:84
  118.9 0.7 copy-done
  119.6 99.4 %reduce-scatter.2.cloned.1.call-done = f32[128,1,512]{0,2,1:T(8,128)} async-done(((f32[4096,1,512]{0,2,1:T(8,128)}), f32[128,1,512]{0,2,1:T(8,128)}) %reduce-scatter.2.cloned.1.call-update) | async-done | bytes 262160 | tf_op jit(solution)/shard_map/reduce_scatter | solution.py:24
  219.1 1.6 convert_element_type.41
  220.7 7.0 %all-to-all-start.1 = ((bf16[8,64,128]{2,1,0:T(8,128)(2,1)}), bf16[8,64,128]{2,1,0:T(8,128)(2,1)S(1)}, u32[]{:S(2)}, u32[]{:S(2)}) async-start(bf16[8,64,128]{2,1,0:T(8,128)(2,1)} %bitcast.11), calls=%async_computation.2 | async-start | bytes 262144 | tf_op jit(solution)/shard_map/all_to_all | solution.py:94
  227.7 9.0 %all-to-all-done.1 = bf16[8,64,128]{2,1,0:T(8,128)(2,1)S(1)} async-done(((bf16[8,64,128]{2,1,0:T(8,128)(2,1)}), bf16[8,64,128]{2,1,0:T(8,128)(2,1)S(1)}, u32[]{:S(2)}, u32[]{:S(2)}) %all-to-all-start.1) | async-done | bytes 131104 | tf_op jit(solution)/shard_map/all_to_all | solution.py:94
  236.7 0.9 fusion.17
  (15 shorter events, 0.2 us)
Async XLA Ops:
  6.5 94.9 %all-gather.2.cloned.1.call-start = ((), (), s32[]{:S(2)}) async-start(), calls=%async_computation.3 | async-start | bytes 4325376 | tf_op jit(solution)/shard_map/all_gather | solution.py:18
  54.3 164.7 %reduce-scatter.2.cloned.1.call-start = ((), (), s32[]{:S(2)}) async-start(), calls=%async_computation.4 | async-start | bytes 8650752 | tf_op jit(solution)/shard_map/reduce_scatter | solution.py:24
  118.9 0.7 copy-start
  118.9 108.8 %copy-start.1 = (s32[128]{0:T(128)S(1)}, s32[128]{0:T(128)}, u32[]{:S(2)}) copy-start(s32[128]{0:T(128)} %param.12) | copy-start | bytes 1540
  220.7 16.1 %all-to-all-start.1 = ((bf16[8,64,128]{2,1,0:T(8,128)(2,1)}), bf16[8,64,128]{2,1,0:T(8,128)(2,1)S(1)}, u32[]{:S(2)}, u32[]{:S(2)}) async-start(bf16[8,64,128]{2,1,0:T(8,128)(2,1)} %bitcast.11), calls=%async_computation.2 | async-start | bytes 262144 | tf_op jit(solution)/shard_map/all_to_all | solution.py:94
Sparse Core Ops, SparseCore 0:
  54.5 46.9 all-gather.1
  119.1 99.9 reduce-scatter.1
where the time goes:
time: 245 us; the launch traced here: 244 us
  waiting for transfers between devices  156 us (64%)
  blocking collectives  39.6 us (16%)
  matrix products  19.3 us (8%)
  between operations  13.5 us (6%)
  starting transfers between devices  7.05 us (3%)
  other arithmetic  5.48 us (2%)
  local copies, waits for them, and re-layouts  3.98 us (2%)
    reduce_scatter x1, waiting for transfers between devices, own_rows(): own = lax.psum_scatter(everything, axis, scatter_dimension=0, tiled=True)  99.4 us
    all_gather x1, waiting for transfers between devices, taken_in(): lax.all_gather(a, axis, axis=dim, tiled=True)  47.1 us
    psum x3, blocking collectives, one_axis_at_a_time(): shard = lax.psum(shard, axis)  21.8 us
    all_to_all x1, blocking collectives, local(): lax.all_to_all(send_rows, 'expert', split_axis=0, concat_axis=0, tiled=True)  17.8 us
    dot_general x1, matrix products, down_terms(): jnp.einsum('hzj,hjs->shz', inner_width, lowering_share, preferred_element...  12 us
    all_to_all x1, waiting for transfers between devices, local(): lax.all_to_all(returning, 'expert', split_axis=0, concat_axis=0, tiled=True)  9.03 us
    all_to_all x1, starting transfers between devices, local(): lax.all_to_all(returning, 'expert', split_axis=0, concat_axis=0, tiled=True)  7.01 us
    dot_general x1, matrix products, add_projections(): jnp.einsum('lrd,lfd->lrf', shard_piece, gate_part, preferred_element_type...  5.4 us
  transfers between devices with their start and end apart: 3, of which 3 were waited for; matrix products, arithmetic and copies ran while one was open for 0% of the time, Pallas kernels for 0%

commit v1 on v0

--- a/solution.py
+++ b/solution.py
@@ -6,6 +6,28 @@
 
 TP = ("tp_0", "tp_1", "tp_2")
 epsilon = 1e-05
+
+
+def cut_along(x, dim, size):
+    before, after = (x.shape[:dim], x.shape[dim + 1 :])
+    return jnp.moveaxis(x.reshape(*before, size, -1, *after), dim, 0)
+
+
+def joined_along(pieces, dim):
+    pieces = jnp.moveaxis(pieces, 0, dim)
+    dims = pieces.shape
+    return pieces.reshape(*dims[:dim], dims[dim] * dims[dim + 1], *dims[dim + 2 :])
+
+
+def swapped_with_each(value, axis, split_dim, concat_dim):
+    size, place = (lax.axis_size(axis), lax.axis_index(axis))
+    parts = cut_along(value, split_dim, size)
+    outs = [parts[place]]
+    for lap in range(1, size):
+        sent = parts[place ^ lap]
+        outs.append(lax.ppermute(sent, axis, [(i, i ^ lap) for i in range(size)]))
+    parts = jnp.stack(outs)[place ^ jnp.arange(size)]
+    return joined_along(parts, concat_dim)
 
 
 def one_axis_at_a_time(shard, axes):
@@ -59,7 +81,7 @@
     send_rows = jnp.einsum(
         "jr,jw->rw", send_hot, normed, preferred_element_type=jnp.float32
     ).astype(jnp.bfloat16)
-    arriving = lax.all_to_all(send_rows, "expert", split_axis=0, concat_axis=0, tiled=True)
+    arriving = swapped_with_each(send_rows, "expert", 0, 0)
     received = arriving.reshape(expert_count, local_count, seat_limit, -1).transpose(1, 0, 2, 3)
     received = received.reshape(local_count, slots, -1)
     empty = jnp.zeros((local_count, slots, ff_share), jnp.float32)

time: 245 us -> 252 us (1.029)
  blocking collectives: 39.6 us -> 21.8 us
  starting transfers between devices: 7.05 us -> 23.4 us
  waiting for transfers between devices: 156 us -> 162 us
    all_to_all x1 -> x0, blocking collectives: 17.8 us -> none  [local(): lax.all_to_all(send_rows, 'expert', split_axis=0, concat_axis=0, tiled=True)]
    ppermute x0 -> x7, starting transfers between devices: none -> 16.4 us  [swapped_with_each(): outs.append(lax.ppermute(sent, axis, [(i, i ^ lap) for i in range(size)]))]
    ppermute x0 -> x7, waiting for transfers between devices: none -> 4.88 us  [swapped_with_each(): outs.append(lax.ppermute(sent, axis, [(i, i ^ lap) for i in range(size)]))]
  transfers between devices with their start and end apart: 3 -> 10, of which waited for: 3 -> 5; matrix products, arithmetic and copies ran while one was open for 0% -> 0% of each run, Pallas kernels for 0% -> 0%
where the time goes in v1:
time: 252 us; the launch traced here: 251 us
  waiting for transfers between devices  162 us (64%)
  starting transfers between devices  23.4 us (9%)
  blocking collectives  21.8 us (9%)
  matrix products  19.3 us (8%)
  between operations  13.5 us (5%)
  other arithmetic  5.5 us (2%)
  local copies, waits for them, and re-layouts  5.27 us (2%)
    reduce_scatter x1, waiting for transfers between devices, own_rows(): own = lax.psum_scatter(everything, axis, scatter_dimension=0, tiled=True)  99.4 us
    all_gather x1, waiting for transfers between devices, taken_in(): lax.all_gather(a, axis, axis=dim, tiled=True)  48.9 us
    psum x3, blocking collectives, one_axis_at_a_time(): shard = lax.psum(shard, axis)  21.8 us
    ppermute x7, starting transfers between devices, swapped_with_each(): outs.append(lax.ppermute(sent, axis, [(i, i ^ lap) for i in range(size)]))  16.4 us
    dot_general x1, matrix products, down_terms(): jnp.einsum('hzj,hjs->shz', inner_width, lowering_share, preferred_element...  12 us
    all_to_all x1, waiting for transfers between devices, local(): lax.all_to_all(returning, 'expert', split_axis=0, concat_axis=0, tiled=True)  9.03 us
    all_to_all x1, starting transfers between devices, local(): lax.all_to_all(returning, 'expert', split_axis=0, concat_axis=0, tiled=True)  7.04 us
    dot_general x1, matrix products, add_projections(): jnp.einsum('lrd,lfd->lrf', shard_piece, gate_part, preferred_element_type...  5.4 us
  transfers between devices with their start and end apart: 10, of which 5 were waited for; matrix products, arithmetic and copies ran while one was open for 0% of the time, Pallas kernels for 0%

profile of v1, /device:TPU:2, one launch (start us, length us, event | category | flops | bytes accessed | tf_op | source)
XLA Modules:
  0.0 251.1 jit_solution(11042070014529382971)
XLA Ops:
  6.5 0.8 copy.19
  7.5 0.1 eq.42
  7.6 0.7 broadcast_in_dim.28
  8.3 0.7 broadcast_compare_fusion
  9.1 0.1 broadcast_in_dim.30
  9.2 0.6 reduce-window.6
  9.8 0.2 slice_reduce_fusion
  10.1 0.7 broadcast_in_dim.31
  10.8 0.1 mul.85
  11.3 0.7 add_select_fusion
  12.1 0.9 fusion.30
  13.0 10.0 %psum.21 = f32[128]{0:T(128)S(1)} all-reduce(f32[128]{0:T(128)S(1)} %fusion.30), channel_id=1, replica_groups=mesh['expert'=8,'tp_0'=4,'tp_1'=4,'tp_2'=2] {'tp_0'}, use_global_device_ids=true, to_apply=%region_7.8 | all-reduce | flops 128 | bytes 1024 | tf_op jit(solution)/shard_map/psum | solution.py:35
  22.9 9.4 %psum.22 = f32[128]{0:T(128)S(1)} all-reduce(f32[128]{0:T(128)S(1)} %psum.21), channel_id=1, replica_groups=mesh['expert'=8,'tp_0'=4,'tp_1'=4,'tp_2'=2] {'tp_1'}, use_global_device_ids=true, to_apply=%region_8.9 | all-reduce | flops 128 | bytes 1024 | tf_op jit(solution)/shard_map/psum | solution.py:35
  32.3 2.5 psum.23
  34.8 0.8 dynamic-slice_convert_fusion
  35.5 1.0 convolution_convert_fusion
  36.6 2.0 collective-permute-start
  38.6 3.3 %collective-permute-start.1 = (bf16[64,128]{1,0:T(8,128)(2,1)S(1)}, bf16[64,128]{1,0:T(8,128)(2,1)S(1)}, u32[]{:S(2)}, u32[]{:S(2)}) collective-permute-start(bf16[64,128]{1,0:T(8,128)(2,1)S(1)} %get-tuple-element.10), channel_id=1, source_target_pairs={{0,64},{32,96},{64,0},{96,32},{128,192},{160,224},{192,128},{224,1... | collective-permute-start | bytes 49160 | tf_op jit(solution)/shard_map/ppermute | solution.py:28
  41.9 6.4 %collective-permute-start.3 = (bf16[64,128]{1,0:T(8,128)(2,1)S(1)}, bf16[64,128]{1,0:T(8,128)(2,1)S(1)}, u32[]{:S(2)}, u32[]{:S(2)}) collective-permute-start(bf16[64,128]{1,0:T(8,128)(2,1)S(1)} %get-tuple-element.8), channel_id=1, source_target_pairs={{0,128},{32,160},{64,192},{96,224},{128,0},{160,32},{192,64},{224,... | collective-permute-start | bytes 49160 | tf_op jit(solution)/shard_map/ppermute | solution.py:28
  48.3 4.7 %collective-permute-start.5 = (bf16[64,128]{1,0:T(8,128)(2,1)S(1)}, bf16[64,128]{1,0:T(8,128)(2,1)S(1)}, u32[]{:S(2)}, u32[]{:S(2)}) collective-permute-start(bf16[64,128]{1,0:T(8,128)(2,1)S(1)} %get-tuple-element.6), channel_id=1, source_target_pairs={{0,192},{32,224},{64,128},{96,160},{128,64},{160,96},{192,0},{224,... | collective-permute-start | bytes 49160 | tf_op jit(solution)/shard_map/ppermute | solution.py:28
  53.0 2.0 collective-permute-done.4
  55.0 2.9 %collective-permute-done.6 = bf16[64,128]{1,0:T(8,128)(2,1)S(1)} collective-permute-done((bf16[64,128]{1,0:T(8,128)(2,1)S(1)}, bf16[64,128]{1,0:T(8,128)(2,1)S(1)}, u32[]{:S(2)}, u32[]{:S(2)}) %collective-permute-start.6) | collective-permute-done | bytes 16416 | tf_op jit(solution)/shard_map/ppermute | solution.py:28
  57.9 1.2 gather_fusion
  59.2 48.9 %all-gather.2.cloned.1.call-done = bf16[1,512,4096]{2,1,0:T(8,128)(2,1)} async-done(((bf16[1,512,128]{2,1,0:T(8,128)(2,1)}), bf16[1,512,4096]{2,1,0:T(8,128)(2,1)}) %all-gather.2.cloned.1.call-update) | async-done | bytes 4194320 | tf_op jit(solution)/shard_map/all_gather | solution.py:40
  108.1 5.4 %fusion.2 = f32[512,448]{0,1:T(8,128)S(1)} fusion(bf16[1,512,4096]{2,1,0:T(8,128)(2,1)} %all-gather.2.cloned.1.call-done, bf16[1,448,4096]{2,1,0:T(8,128)(2,1)} %param.13), kind=kOutput, calls=%fused_computation.4 | convolution fusion | flops 1879048192 | bytes 8781824 | tf_op jit(solution)/shard_map/lrd,lfd->lrf/dot_general | solution.py:93
  113.5 12.0 %convolution_bitcast_fusion = f32[4096,1,512]{0,2,1:T(8,128)} fusion(bf16[1,448,4096]{2,1,0:T(8,128)(2,1)} %param.15, bf16[1,448,4096]{2,1,0:T(8,128)(2,1)} %param.14, bf16[1,512,4096]{2,1,0:T(8,128)(2,1)} %all-gather.2.cloned.1.call-done, f32[512,448]{0,1:T(8,128)S(1)} %fusion.2), kind=kOutput, calls=%fused_computation.1 | convolution fusion | flops 3759472640 | bytes 20840448 | tf_op jit(solution)/shard_map/hzj,hjs->shz/dot_general | solution.py:106
  125.5 0.7 copy-done
  126.2 99.4 %reduce-scatter.2.cloned.1.call-done = f32[128,1,512]{0,2,1:T(8,128)} async-done(((f32[4096,1,512]{0,2,1:T(8,128)}), f32[128,1,512]{0,2,1:T(8,128)}) %reduce-scatter.2.cloned.1.call-update) | async-done | bytes 262160 | tf_op jit(solution)/shard_map/reduce_scatter | solution.py:46
  225.6 1.6 convert_element_type.41
  227.2 7.0 %all-to-all-start = ((bf16[8,64,128]{2,1,0:T(8,128)(2,1)}), bf16[8,64,128]{2,1,0:T(8,128)(2,1)S(1)}, u32[]{:S(2)}, u32[]{:S(2)}) async-start(bf16[8,64,128]{2,1,0:T(8,128)(2,1)} %bitcast.26), calls=%async_computation.1 | async-start | bytes 262144 | tf_op jit(solution)/shard_map/all_to_all | solution.py:116
  234.3 9.0 %all-to-all-done = bf16[8,64,128]{2,1,0:T(8,128)(2,1)S(1)} async-done(((bf16[8,64,128]{2,1,0:T(8,128)(2,1)}), bf16[8,64,128]{2,1,0:T(8,128)(2,1)S(1)}, u32[]{:S(2)}, u32[]{:S(2)}) %all-to-all-start) | async-done | bytes 131104 | tf_op jit(solution)/shard_map/all_to_all | solution.py:116
  243.3 0.9 fusion.17
  (39 shorter events, 0.9 us)
Async XLA Ops:
  6.5 101.5 %all-gather.2.cloned.1.call-start = ((), (), s32[]{:S(2)}) async-start(), calls=%async_computation.2 | async-start | bytes 4325376 | tf_op jit(solution)/shard_map/all_gather | solution.py:40
  36.6 11.7 %collective-permute-start = (bf16[64,128]{1,0:T(8,128)(2,1)S(1)}, bf16[64,128]{1,0:T(8,128)(2,1)S(1)}, u32[]{:S(2)}, u32[]{:S(2)}) collective-permute-start(bf16[64,128]{1,0:T(8,128)(2,1)S(1)} %get-tuple-element.11), channel_id=1, source_target_pairs={{0,32},{32,0},{64,96},{96,64},{128,160},{160,128},{192,224},{224,1... | collective-permute-start | bytes 49160 | tf_op jit(solution)/shard_map/ppermute | solution.py:28
  38.6 14.4 %collective-permute-start.1 = (bf16[64,128]{1,0:T(8,128)(2,1)S(1)}, bf16[64,128]{1,0:T(8,128)(2,1)S(1)}, u32[]{:S(2)}, u32[]{:S(2)}) collective-permute-start(bf16[64,128]{1,0:T(8,128)(2,1)S(1)} %get-tuple-element.10), channel_id=1, source_target_pairs={{0,64},{32,96},{64,0},{96,32},{128,192},{160,224},{192,128},{224,1... | collective-permute-start | bytes 49160 | tf_op jit(solution)/shard_map/ppermute | solution.py:28
  41.9 11.1 %collective-permute-start.2 = (bf16[64,128]{1,0:T(8,128)(2,1)S(1)}, bf16[64,128]{1,0:T(8,128)(2,1)S(1)}, u32[]{:S(2)}, u32[]{:S(2)}) collective-permute-start(bf16[64,128]{1,0:T(8,128)(2,1)S(1)} %get-tuple-element.9), channel_id=1, source_target_pairs={{0,96},{32,64},{64,32},{96,0},{128,224},{160,192},{192,160},{224,1... | collective-permute-start | bytes 49160 | tf_op jit(solution)/shard_map/ppermute | solution.py:28
  41.9 11.2 %collective-permute-start.3 = (bf16[64,128]{1,0:T(8,128)(2,1)S(1)}, bf16[64,128]{1,0:T(8,128)(2,1)S(1)}, u32[]{:S(2)}, u32[]{:S(2)}) collective-permute-start(bf16[64,128]{1,0:T(8,128)(2,1)S(1)} %get-tuple-element.8), channel_id=1, source_target_pairs={{0,128},{32,160},{64,192},{96,224},{128,0},{160,32},{192,64},{224,... | collective-permute-start | bytes 49160 | tf_op jit(solution)/shard_map/ppermute | solution.py:28
  48.2 6.7 %collective-permute-start.4 = (bf16[64,128]{1,0:T(8,128)(2,1)S(1)}, bf16[64,128]{1,0:T(8,128)(2,1)S(1)}, u32[]{:S(2)}, u32[]{:S(2)}) collective-permute-start(bf16[64,128]{1,0:T(8,128)(2,1)S(1)} %get-tuple-element.7), channel_id=1, source_target_pairs={{0,160},{32,128},{64,224},{96,192},{128,32},{160,0},{192,96},{224,... | collective-permute-start | bytes 49160 | tf_op jit(solution)/shard_map/ppermute | solution.py:28
  48.3 6.7 %collective-permute-start.5 = (bf16[64,128]{1,0:T(8,128)(2,1)S(1)}, bf16[64,128]{1,0:T(8,128)(2,1)S(1)}, u32[]{:S(2)}, u32[]{:S(2)}) collective-permute-start(bf16[64,128]{1,0:T(8,128)(2,1)S(1)} %get-tuple-element.6), channel_id=1, source_target_pairs={{0,192},{32,224},{64,128},{96,160},{128,64},{160,96},{192,0},{224,... | collective-permute-start | bytes 49160 | tf_op jit(solution)/shard_map/ppermute | solution.py:28
  53.0 5.0 %collective-permute-start.6 = (bf16[64,128]{1,0:T(8,128)(2,1)S(1)}, bf16[64,128]{1,0:T(8,128)(2,1)S(1)}, u32[]{:S(2)}, u32[]{:S(2)}) collective-permute-start(bf16[64,128]{1,0:T(8,128)(2,1)S(1)} %get-tuple-element.5), channel_id=1, source_target_pairs={{0,224},{32,192},{64,160},{96,128},{128,96},{160,64},{192,32},{224... | collective-permute-start | bytes 49160 | tf_op jit(solution)/shard_map/ppermute | solution.py:28
  59.1 166.5 %reduce-scatter.2.cloned.1.call-start = ((), (), s32[]{:S(2)}) async-start(), calls=%async_computation.3 | async-start | bytes 8650752 | tf_op jit(solution)/shard_map/reduce_scatter | solution.py:46
  125.5 0.7 copy-start
  125.5 108.8 %copy-start.1 = (s32[128]{0:T(128)S(1)}, s32[128]{0:T(128)}, u32[]{:S(2)}) copy-start(s32[128]{0:T(128)} %param.12) | copy-start | bytes 1540
  227.2 16.1 %all-to-all-start = ((bf16[8,64,128]{2,1,0:T(8,128)(2,1)}), bf16[8,64,128]{2,1,0:T(8,128)(2,1)S(1)}, u32[]{:S(2)}, u32[]{:S(2)}) async-start(bf16[8,64,128]{2,1,0:T(8,128)(2,1)} %bitcast.26), calls=%async_computation.1 | async-start | bytes 262144 | tf_op jit(solution)/shard_map/all_to_all | solution.py:116
Sparse Core Ops, SparseCore 0:
  59.3 48.7 all-gather.1
  125.7 99.9 reduce-scatter.1
